TPU v7x, 256 devices: a whole 4x4x8 slice. The times are simulated.
256 devices in a mesh: dp: 4 (over x), expert: 64 (over y, z, core).
Axes of the slice: x: 4, y: 4, z: 8, core: 2. Of those that a mesh axis runs over, the one named last changes fastest.
Arguments:
- hidden: bfloat16 [4, 4096, 2, 2048], P('dp', 'expert'), may hold values from -6 to 6
- queries: bfloat16 [4, 4096, 2, 4096], P('dp', 'expert'), may hold values from -45 to 45
- latents: bfloat16 [4, 4096, 2, 512], P('dp', 'expert'), may hold values from -165 to 165
- mem_latents: bfloat16 [4, 32, 2, 512], P('dp'), may hold values from -6 to 6
- lengths: int32 [4, 2], P('dp'), may hold values from 2048 to 4096
- ids: int32 [4, 4096, 2, 6], P('dp', 'expert'), may hold values from 0 to 63, all different within a row; in each aligned block of 128 rows (0 to 127, 128 to 255, ..., all dimensions but the last counted through in order) at most 14 rows name the same one
- gates: bfloat16 [4, 4096, 2, 6], P('dp', 'expert'), may hold values from 0.049804688 to 0.5
- norm_gain: bfloat16 [2048], replicated, may hold values from 0.25 to 1.75
- w_uv: bfloat16 [8, 512, 128], P('dp'), may hold values from -0.25 to 0.25
- w_out: bfloat16 [1024, 2048], P('dp'), may hold values from -0.1875 to 0.1875
- w_gate: bfloat16 [64, 2048, 704], P('expert'), may hold values from -0.125 to 0.125
- w_up: bfloat16 [64, 2048, 704], P('expert'), may hold values from -0.125 to 0.125
- w_down: bfloat16 [64, 704, 2048], P('expert'), may hold values from -0.21875 to 0.21875
Outputs:
- layer_out: bfloat16 [4, 4096, 2, 2048], P('dp', 'expert')
Inputs may be any that keep to these rules, and one draw needn't show every extreme that they name: `ids`: each row names 6 different experts; the rows of one device (aligned blocks of 128 rows in the order of the leading dimensions) name any one expert at most 14 times, a bound that some block reaches.
All inputs are finite; a program needn't handle non-finite values.
Results may differ from a plain program's by a relative error of at most 0.007.
Values may be sent and summed in bfloat16 or wider, within the bound.
A program may use at most 128 MiB of HBM per device.

v0:
```python
import jax
import jax.numpy as jnp
from jax import lax
from jax.sharding import PartitionSpec as P

score_scale = 192.0 ** (-0.5)
norm_eps = 1e-06


def sent_to_all(shard, axis):
    devices = lax.axis_size(axis)
    return lax.all_to_all(
        jnp.broadcast_to(shard[None], (devices, *shard.shape)), axis, 0, 0, tiled=True
    )


def joined_along(blocks, dim):
    dims = list(blocks.shape[1:])
    dims[dim] *= blocks.shape[0]
    return jnp.moveaxis(blocks, 0, dim).reshape(dims)


def gather_directly(shard, axis, dim):
    blocks = sent_to_all(shard, axis)
    return joined_along(blocks, dim)


def shards(
    hidden,
    queries,
    latents,
    mem_latents,
    lengths,
    ids,
    gates,
    norm_gain,
    w_uv,
    w_out,
    w_gate,
    w_up,
    w_down,
):
    local_len = hidden.shape[1]
    seq_count = hidden.shape[2]
    model_width = hidden.shape[3]
    latent_dim = latents.shape[3]
    head_count = queries.shape[3] // latent_dim
    row_count = local_len * seq_count
    owner_count = lax.axis_size("expert")
    shard_index = lax.axis_index("expert")
    own_pos = shard_index * local_len + jnp.arange(local_len, dtype=jnp.int32)
    query_rows = queries[0].reshape(local_len, seq_count, head_count, latent_dim)
    memory = mem_latents[0]
    seq_limit = lengths[0]
    mem_scores = (
        jnp.einsum("tshl,msl->shtm", query_rows, memory, preferred_element_type=jnp.float32)
        * score_scale
    )
    first_max = jnp.max(mem_scores, axis=3)
    mem_weights = jnp.exp(mem_scores - first_max[..., None])
    first_sum = jnp.sum(mem_weights, axis=3)
    first_acc = jnp.einsum(
        "shtm,msl->tshl",
        mem_weights.astype(jnp.bfloat16),
        memory,
        preferred_element_type=jnp.float32,
    )

    def fold_step(carry, portion):
        old_max, old_sum, old_acc = carry
        key_rows = portion[0]
        key_pos = jnp.arange(key_rows.shape[0], dtype=jnp.int32)
        scores = (
            jnp.einsum("tshl,jsl->shtj", query_rows, key_rows, preferred_element_type=jnp.float32)
            * score_scale
        )
        causal = key_pos[None, :] <= own_pos[:, None]
        inside = key_pos[None, :] < seq_limit[:, None]
        visible = causal[None, None, :, :] & inside[:, None, None, :]
        scores = jnp.where(visible, scores, -jnp.inf)
        new_max = jnp.maximum(old_max, jnp.max(scores, axis=3))
        weights = jnp.exp(scores - new_max[..., None])
        factor = jnp.exp(old_max - new_max)
        new_sum = old_sum * factor + jnp.sum(weights, axis=3)
        contrib = jnp.einsum(
            "shtj,jsl->tshl",
            weights.astype(jnp.bfloat16),
            key_rows,
            preferred_element_type=jnp.float32,
        )
        new_acc = old_acc * jnp.transpose(factor, (2, 0, 1))[..., None] + contrib
        return (new_max, new_sum, new_acc)

    portion = lax.all_gather(latents, "expert", axis=1, tiled=True)
    last_pos = jnp.max(own_pos)
    final_max, final_sum, final_acc = lax.cond(
        jnp.int32(0) <= last_pos,
        lambda state: fold_step(state, portion),
        lambda state: state,
        (first_max, first_sum, first_acc),
    )
    attended = (final_acc / jnp.transpose(final_sum, (2, 0, 1))[..., None]).astype(jnp.bfloat16)
    values = jnp.einsum(
        "tshl,hlv->tshv",
        attended,
        gather_directly(w_uv, "dp", 0),
        preferred_element_type=jnp.float32,
    ).astype(jnp.bfloat16)
    flat_values = values.reshape(row_count, -1)
    attn_out = jnp.dot(
        flat_values,
        lax.all_gather(w_out, "dp", axis=0, tiled=True),
        preferred_element_type=jnp.float32,
    )
    residual = hidden[0].reshape(row_count, model_width).astype(jnp.float32) + attn_out
    mean_square = jnp.mean(residual * residual, axis=-1, keepdims=True)
    normed = (residual * lax.rsqrt(mean_square + norm_eps) * norm_gain.astype(jnp.float32)).astype(
        jnp.bfloat16
    )
    experts_here = w_gate.shape[0]
    expert_count = owner_count * experts_here
    top_count = ids.shape[3]
    capacity = min(row_count, row_count * top_count // expert_count + 2)
    flat_ids = ids[0].reshape(row_count * top_count)
    onehot = (flat_ids[:, None] == jnp.arange(expert_count, dtype=jnp.int32)[None, :]).astype(
        jnp.int32
    )
    before = jnp.cumsum(onehot, axis=0) - onehot
    slot_within = jnp.sum(before * onehot, axis=1)
    slot_index = (flat_ids * capacity + slot_within).reshape(row_count, top_count)
    matching = (
        jnp.arange(expert_count * capacity, dtype=jnp.int32)[:, None, None]
        == slot_index[None, :, :]
    )
    placing = jnp.any(matching, axis=2).astype(jnp.bfloat16)
    gate_rows = gates[0].reshape(row_count, top_count).astype(jnp.float32)
    mixing = jnp.sum(jnp.where(matching, gate_rows[None, :, :], jnp.float32(0.0)), axis=2).astype(
        jnp.bfloat16
    )
    outgoing = jnp.dot(placing, normed, preferred_element_type=jnp.float32).astype(jnp.bfloat16)
    outgoing = outgoing.reshape(owner_count, experts_here, capacity, model_width)
    incoming = lax.all_to_all(outgoing, "expert", split_axis=0, concat_axis=0, tiled=True)
    gate_h = jnp.einsum("necd,edf->necf", incoming, w_gate, preferred_element_type=jnp.float32)
    up_h = jnp.einsum("necd,edf->necf", incoming, w_up, preferred_element_type=jnp.float32)
    act = (jax.nn.silu(gate_h) * up_h).astype(jnp.bfloat16)
    produced = jnp.einsum("necf,efd->necd", act, w_down, preferred_element_type=jnp.float32).astype(
        jnp.bfloat16
    )
    returned = lax.all_to_all(produced, "expert", split_axis=0, concat_axis=0, tiled=True)
    combined_rows = returned.reshape(expert_count * capacity, model_width)
    routed = jnp.einsum("st,sd->td", mixing, combined_rows, preferred_element_type=jnp.float32)
    layer_out = (residual + routed).astype(jnp.bfloat16)
    return layer_out.reshape(1, local_len, seq_count, model_width)


def solution(mesh):
    return jax.shard_map(
        shards,
        mesh=mesh,
        in_specs=(
            P("dp", "expert", None, None),
            P("dp", "expert", None, None),
            P("dp", "expert", None, None),
            P("dp", None, None, None),
            P("dp", None),
            P("dp", "expert", None, None),
            P("dp", "expert", None, None),
            P(),
            P("dp", None, None),
            P("dp", None),
            P("expert", None, None),
            P("expert", None, None),
            P("expert", None, None),
        ),
        out_specs=P("dp", "expert", None, None),
        check_vma=False,
    )
```

profile of v0, /device:TPU:1, one launch (start us, length us, event | category | flops | bytes accessed | tf_op | source)
XLA Modules:
  0.0 415.4 jit_solution(3627106416608245663)
XLA Ops:
  6.5 1.7 copy.55
  9.0 2.1 broadcast_in_dim.29
  11.1 4.8 %all-to-all-start = ((bf16[4,2,512,128]{3,2,1,0:T(8,128)(2,1)}), bf16[4,2,512,128]{3,2,1,0:T(8,128)(2,1)}, u32[]{:S(2)}, u32[]{:S(2)}) async-start(bf16[4,2,512,128]{3,2,1,0:T(8,128)(2,1)} %broadcast_in_dim.29), calls=%async_computation | async-start | bytes 2097152 | tf_op jit(solution)/shard_map/all_to_all | solution.py:12
  16.4 2.6 reshape.151
  20.3 1.1 reshape.142
  21.5 1.8 reduce-window.6
  23.9 2.5 fusion.69
  26.7 2.7 convolution_bitcast_fusion
  29.9 67.4 %all-gather.3.cloned.1.call-done = bf16[1,4096,2,512]{3,1,2,0:T(8,128)(2,1)} async-done(((bf16[1,64,2,512]{3,1,2,0:T(8,128)(2,1)}), bf16[1,4096,2,512]{3,1,2,0:T(8,128)(2,1)}) %all-gather.3.cloned.1.call-update) | async-done | bytes 8388624 | tf_op jit(solution)/shard_map/all_gather | solution.py:94
  97.3 38.6 %conditional.1 = ((f32[2,8,64]{2,1,0:T(8,128)S(1)}, f32[64,2,8,512]{3,0,2,1:T(8,128)})) conditional(s32[]{:T(128)} %convert_element_type.74, (f32[2,8,64]{2,1,0:T(8,128)S(1)}, f32[64,2,8,512]{3,0,2,1:T(8,128)}) %tuple.12, (s32[64]{0:T(128)S(1)}, s32[1,2]{1,0:T(1,128)}, bf16[1,4096,2,512]{3,1,2,0:T(8,128)(2,1)}, bf16[64,2,8,512]{3,2,1,0:T(8,128)(2,1)}, ...), branch_computations={%region_3.0_spmd, %region_4.7_spmd} | conditional | flops 8637918208 | bytes 75047200 | solution.py:96
  97.5 0.7 iota_compare_fusion.1
  98.6 15.8 %fusion.2 = (f32[2,8,64]{2,1,0:T(8,128)}, f32[2,4096,64,8]{1,2,3,0:T(8,128)}) fusion(pred[2,64,4096]{2,1,0:T(8,128)(4,1)S(1)} %broadcast_and_fusion, bf16[64,2,8,512]{3,2,1,0:T(8,128)(2,1)} %get-tuple-element.57, bf16[1,4096,2,512]{3,1,2,0:T(8,128)(2,1)} %get-tuple-element.27), kind=kOutput, calls=%fused_computation.4 | convolution fusion | flops 4307549184 | bytes 26742784 | tf_op jit(solution)/shard_map/cond/branch_1_fun/tshl,jsl->shtj/dot_general | solution.py:74
  114.4 0.7 fusion.17
  115.1 12.4 %bitcast_add_fusion = f32[64,2,8,512]{3,0,2,1:T(8,128)} fusion(f32[64,2,8,512]{3,0,2,1:T(8,128)} %get-tuple-element.29, bf16[1,4096,2,512]{3,1,2,0:T(8,128)(2,1)} %get-tuple-element.27, f32[2,4096,64,8]{1,2,3,0:T(8,128)} %get-tuple-element.61, f32[2,8,64]{2,1,0:T(8,128)S(1)} %get-tuple-element.59, pred[2,64,4096]{2,1,0:T(8,128)(4,1)S(1)} %broadcast_and_fusion, ...), kind=kOutput, calls=%fused_computation.13 | convolution fusion | flops 4312793088 | bytes 29892608 | tf_op jit(solution)/shard_map/cond/branch_1_fun/shtj,jsl->tshl/dot_general | solution.py:85
  127.5 8.4 %fusion.1 = f32[2,8,64]{2,1,0:T(8,128)S(1)} fusion(f32[2,4096,64,8]{1,2,3,0:T(8,128)} %get-tuple-element.61, f32[2,8,64]{2,1,0:T(8,128)S(1)} %get-tuple-element.59, pred[2,64,4096]{2,1,0:T(8,128)(4,1)S(1)} %broadcast_and_fusion), kind=kLoop, calls=%fused_computation.3 | loop fusion | flops 16776192 | bytes 17309696 | tf_op jit(solution)/shard_map/cond/branch_1_fun/reduce_sum | solution.py:84
  135.9 2.4 fusion.48
  138.5 7.6 %all-gather.5.cloned.1.call-done = bf16[1024,2048]{1,0:T(8,128)(2,1)} async-done(((bf16[256,2048]{1,0:T(8,128)(2,1)}), bf16[1024,2048]{1,0:T(8,128)(2,1)}) %all-gather.5.cloned.1.call-update) | async-done | bytes 4194320 | tf_op jit(solution)/shard_map/all_gather | solution.py:112
  146.1 3.3 multiply_reduce_fusion
  149.4 1.0 copy-done.1
  150.4 3.0 convolution_convert_fusion
  153.4 6.0 %reshape.134 = bf16[64,1,14,2048]{3,2,0,1:T(8,128)(2,1)} reshape(bf16[896,2048]{1,0:T(8,128)(2,1)} %convolution_convert_fusion) | data formatting | bytes 7340032 | tf_op jit(solution)/shard_map/reshape | solution.py:141
  159.4 107.3 %all_to_all.15 = bf16[64,1,14,2048]{3,2,1,0:T(8,128)(2,1)S(1)} all-to-all(bf16[64,1,14,2048]{3,2,1,0:T(8,128)(2,1)} %bitcast.151), channel_id=1, replica_groups=mesh['dp'=4,'expert'=64] {'expert'}, dimensions={0} | all-to-all | bytes 7340032 | tf_op jit(solution)/shard_map/all_to_all | solution.py:142
  266.7 1.9 copy-done.2
  268.6 8.7 %fusion.22 = f32[64,14,704]{2,0,1:T(8,128)} fusion(bf16[64,1,14,2048]{3,2,1,0:T(8,128)(2,1)S(1)} %all_to_all.15, bf16[1,2048,704]{1,2,0:T(8,128)(2,1)S(1)} %copy-done.7), kind=kOutput, calls=%fused_computation.25 | convolution fusion | flops 2583691264 | bytes 9076736 | tf_op jit(solution)/shard_map/necd,edf->necf/dot_general | solution.py:143
  277.3 12.9 %convert_bitcast_fusion = bf16[64,1,14,2048]{3,0,2,1:T(8,128)(2,1)} fusion(bf16[1,704,2048]{2,1,0:T(8,128)(2,1)S(1)} %copy-done, bf16[1,2048,704]{1,2,0:T(8,128)(2,1)} %param.26, bf16[64,1,14,2048]{3,2,1,0:T(8,128)(2,1)} %copy-done.2, f32[64,14,704]{2,0,1:T(8,128)} %fusion.22), kind=kOutput, calls=%fused_computation.27 | convolution fusion | flops 5173002240 | bytes 15630336 | tf_op jit(solution)/shard_map/necf,efd->necd/dot_general | solution.py:146
  290.2 6.0 %copy.68 = bf16[64,1,14,2048]{3,2,1,0:T(8,128)(2,1)} copy(bf16[64,1,14,2048]{3,0,2,1:T(8,128)(2,1)} %convert_bitcast_fusion) | data formatting | bytes 7340032 | tf_op jit(solution)/shard_map/convert_element_type | solution.py:146
  296.2 6.2 %all-to-all-start.2 = ((bf16[64,1,14,2048]{3,2,1,0:T(8,128)(2,1)}), bf16[64,1,14,2048]{3,2,1,0:T(8,128)(2,1)}, u32[]{:S(2)}, u32[]{:S(2)}) async-start(bf16[64,1,14,2048]{3,2,1,0:T(8,128)(2,1)} %copy.68), calls=%async_computation.2 | async-start | bytes 8388608 | tf_op jit(solution)/shard_map/all_to_all | solution.py:149
  302.6 1.0 select_reduce_fusion
  303.6 94.6 %all-to-all-done.2 = bf16[64,1,14,2048]{3,2,1,0:T(8,128)(2,1)} async-done(((bf16[64,1,14,2048]{3,2,1,0:T(8,128)(2,1)}), bf16[64,1,14,2048]{3,2,1,0:T(8,128)(2,1)}, u32[]{:S(2)}, u32[]{:S(2)}) %all-to-all-start.2) | async-done | bytes 3670048 | tf_op jit(solution)/shard_map/all_to_all | solution.py:149
  398.3 6.0 %reshape.140 = bf16[896,2048]{1,0:T(8,128)(2,1)} reshape(bf16[64,1,14,2048]{3,2,1,0:T(8,128)(2,1)} %all-to-all-done.2) | data formatting | bytes 7340032 | tf_op jit(solution)/shard_map/reshape | solution.py:150
  404.2 3.1 fusion.34
  407.4 1.1 reshape.141
  (43 shorter events, 4.1 us)
Async XLA Ops:
  6.5 270.8 %copy-start = (bf16[1,704,2048]{2,1,0:T(8,128)(2,1)S(1)}, bf16[1,704,2048]{2,1,0:T(8,128)(2,1)}, u32[]{:S(2)}) copy-start(bf16[1,704,2048]{2,1,0:T(8,128)(2,1)} %param.27) | copy-start | bytes 8650756
  6.5 9.4 %copy-start.4 = (s32[1,64,2,6]{1,2,3,0:T(2,128)S(1)}, s32[1,64,2,6]{1,2,3,0:T(2,128)}, u32[]{:S(2)}) copy-start(s32[1,64,2,6]{1,2,3,0:T(2,128)} %param.20) | copy-start | bytes 9220
  6.5 13.8 %copy-start.3 = (bf16[1,64,2,2048]{3,2,1,0:T(2,128)(2,1)S(1)}, bf16[1,64,2,2048]{3,2,1,0:T(2,128)(2,1)}, u32[]{:S(2)}) copy-start(bf16[1,64,2,2048]{3,2,1,0:T(2,128)(2,1)} %param.15) | copy-start | bytes 1572868
  6.5 90.8 %all-gather.3.cloned.1.call-start = ((), (), s32[]{:S(2)}) async-start(), calls=%async_computation.3 | async-start | bytes 8519680 | tf_op jit(solution)/shard_map/all_gather | solution.py:94
  8.3 137.8 %all-gather.5.cloned.1.call-start = ((), (), s32[]{:S(2)}) async-start(), calls=%async_computation.4 | async-start | bytes 5242880 | tf_op jit(solution)/shard_map/all_gather | solution.py:112
  11.1 124.8 %all-to-all-start = ((bf16[4,2,512,128]{3,2,1,0:T(8,128)(2,1)}), bf16[4,2,512,128]{3,2,1,0:T(8,128)(2,1)}, u32[]{:S(2)}, u32[]{:S(2)}) async-start(bf16[4,2,512,128]{3,2,1,0:T(8,128)(2,1)} %broadcast_in_dim.29), calls=%async_computation | async-start | bytes 2097152 | tf_op jit(solution)/shard_map/all_to_all | solution.py:12
  16.0 10.7 %copy-start.5 = (bf16[2048]{0:T(1024)(128)(2,1)S(1)}, bf16[2048]{0:T(1024)(128)(2,1)}, u32[]{:S(2)}) copy-start(bf16[2048]{0:T(1024)(128)(2,1)} %param.22) | copy-start | bytes 12292
  149.4 1.0 copy-start.1
  159.4 109.2 %copy-start.7 = (bf16[1,2048,704]{1,2,0:T(8,128)(2,1)S(1)}, bf16[1,2048,704]{1,2,0:T(8,128)(2,1)}, u32[]{:S(2)}) copy-start(bf16[1,2048,704]{1,2,0:T(8,128)(2,1)} %param.25) | copy-start | bytes 8650756
  266.7 1.9 copy-start.2
  296.2 6.2 %copy-start.6 = (bf16[1,64,2,6]{1,2,3,0:T(2,128)(2,1)S(1)}, bf16[1,64,2,6]{1,2,3,0:T(2,128)(2,1)}, u32[]{:S(2)}) copy-start(bf16[1,64,2,6]{1,2,3,0:T(2,128)(2,1)} %param.21) | copy-start | bytes 4612
  296.2 102.0 %all-to-all-start.2 = ((bf16[64,1,14,2048]{3,2,1,0:T(8,128)(2,1)}), bf16[64,1,14,2048]{3,2,1,0:T(8,128)(2,1)}, u32[]{:S(2)}, u32[]{:S(2)}) async-start(bf16[64,1,14,2048]{3,2,1,0:T(8,128)(2,1)} %copy.68), calls=%async_computation.2 | async-start | bytes 8388608 | tf_op jit(solution)/shard_map/all_to_all | solution.py:149
Sparse Core Ops, SparseCore 0:
  10.1 87.1 all-gather.2
  99.1 46.9 all-gather.4
where the time goes:
time: 416 us; the launch traced here: 415 us
  waiting for transfers between devices  170 us (41%)
  blocking collectives  107 us (26%)
  matrix products  66.9 us (16%)
  local copies, waits for them, and re-layouts  30.9 us (7%)
  other arithmetic  14.6 us (4%)
  between operations  14.2 us (3%)
  starting transfers between devices  11.1 us (3%)
    all_to_all x1, blocking collectives, shards(): lax.all_to_all(outgoing, 'expert', split_axis=0, concat_axis=0, tiled=True)  107 us
    all_to_all x1, waiting for transfers between devices, shards(): lax.all_to_all(produced, 'expert', split_axis=0, concat_axis=0, tiled=True)  94.6 us
    all_gather x1, waiting for transfers between devices, shards(): portion = lax.all_gather(latents, 'expert', axis=1, tiled=True)  67.4 us
    dot_general x1, matrix products, fold_step(): jnp.einsum('tshl,jsl->shtj', query_rows, key_rows, preferred_element_type...  15.8 us
    dot_general x1, matrix products, shards(): jnp.einsum('necf,efd->necd', act, w_down, preferred_element_type=jnp.floa...  12.9 us
    dot_general x1, matrix products, fold_step(): jnp.einsum('shtj,jsl->tshl', weights.astype(jnp.bfloat16), key_rows, pref...  12.4 us
    dot_general x1, matrix products, shards(): jnp.einsum('necd,edf->necf', incoming, w_gate, preferred_element_type=jnp...  8.67 us
    reduce_sum x1, other arithmetic, fold_step(): new_sum = old_sum * factor + jnp.sum(weights, axis=3)  8.39 us
  transfers between devices with their start and end apart: 4, of which 3 were waited for; matrix products, arithmetic and copies ran while one was open for 14% of the time, Pallas kernels for 0%

commit v1 on v0

--- a/solution.py
+++ b/solution.py
@@ -91,7 +91,10 @@
         new_acc = old_acc * jnp.transpose(factor, (2, 0, 1))[..., None] + contrib
         return (new_max, new_sum, new_acc)
 
-    portion = lax.all_gather(latents, "expert", axis=1, tiled=True)
+    n_dev = lax.axis_size("expert")
+    pieces = jnp.stack([latents for _ in range(n_dev)])
+    pieces = lax.all_to_all(pieces, "expert", split_axis=0, concat_axis=0)
+    portion = jnp.concatenate(pieces, axis=1)
     last_pos = jnp.max(own_pos)
     final_max, final_sum, final_acc = lax.cond(
         jnp.int32(0) <= last_pos,

time: 416 us -> 532 us (1.28)
  waiting for transfers between devices: 170 us -> 270 us
  starting transfers between devices: 11.1 us -> 23.9 us
  local copies, waits for them, and re-layouts: 30.9 us -> 43.6 us
  matrix products: 66.9 us -> 61.3 us
    all_to_all x0 -> x1, waiting for transfers between devices: none -> 175 us  [shards(): pieces = lax.all_to_all(pieces, 'expert', split_axis=0, concat_axis=0)]
    all_gather x1 -> x0, waiting for transfers between devices: 67.4 us -> none  [shards(): portion = lax.all_gather(latents, 'expert', axis=1, tiled=True)]
    all_to_all x0 -> x1, starting transfers between devices: none -> 13.5 us  [shards(): pieces = lax.all_to_all(pieces, 'expert', split_axis=0, concat_axis=0)]
    another operation x0 -> x3, local copies, waits for them, and re-layouts: none -> 13 us
    all_gather x1, waiting for transfers between devices: 7.61 us -> 0.02 us  [shards(): lax.all_gather(w_out, 'dp', axis=0, tiled=True)]
  transfers between devices with their start and end apart: 4 -> 4, of which waited for: 3 -> 2; matrix products, arithmetic and copies ran while one was open for 14% -> 11% of each run, Pallas kernels for 0% -> 0%
where the time goes in v1:
time: 532 us; the launch traced here: 531 us
  waiting for transfers between devices  270 us (51%)
  blocking collectives  102 us (19%)
  matrix products  61.3 us (12%)
  local copies, waits for them, and re-layouts  43.6 us (8%)
  starting transfers between devices  23.9 us (4%)
  other arithmetic  15.2 us (3%)
  between operations  14.3 us (3%)
    all_to_all x1, waiting for transfers between devices, shards(): pieces = lax.all_to_all(pieces, 'expert', split_axis=0, concat_axis=0)  175 us
    all_to_all x1, blocking collectives, shards(): lax.all_to_all(outgoing, 'expert', split_axis=0, concat_axis=0, tiled=True)  102 us
    all_to_all x1, waiting for transfers between devices, shards(): lax.all_to_all(produced, 'expert', split_axis=0, concat_axis=0, tiled=True)  94.6 us
    dot_general x1, matrix products, fold_step(): jnp.einsum('tshl,jsl->shtj', query_rows, key_rows, preferred_element_type...  15.3 us
    all_to_all x1, starting transfers between devices, shards(): pieces = lax.all_to_all(pieces, 'expert', split_axis=0, concat_axis=0)  13.5 us
    dot_general x1, matrix products, shards(): jnp.einsum('necf,efd->necd', act, w_down, preferred_element_type=jnp.floa...  12.9 us
  transfers between devices with their start and end apart: 4, of which 2 were waited for; matrix products, arithmetic and copies ran while one was open for 11% of the time, Pallas kernels for 0%

profile of v1, /device:TPU:1, one launch (start us, length us, event | category | flops | bytes accessed | tf_op | source)
XLA Modules:
  0.0 530.7 jit_solution(11339926104315359042)
XLA Ops:
  6.5 1.1 copy.56
  7.6 4.3 stack.2
  11.9 13.5 %all-to-all-start = ((bf16[64,1,64,2,512]{4,2,3,1,0:T(8,128)(2,1)}), bf16[64,1,64,2,512]{4,2,3,1,0:T(8,128)(2,1)}, u32[]{:S(2)}, u32[]{:S(2)}) async-start(bf16[64,1,64,2,512]{4,2,3,1,0:T(8,128)(2,1)} %stack.2), calls=%async_computation | async-start | bytes 16777216 | tf_op jit(solution)/shard_map/all_to_all | solution.py:96
  26.5 2.6 reshape.154
  30.4 1.1 reshape.145
  31.6 1.8 reduce-window.6
  34.0 2.5 fusion.65
  36.5 174.6 %all-to-all-done = bf16[64,1,64,2,512]{4,2,3,1,0:T(8,128)(2,1)} async-done(((bf16[64,1,64,2,512]{4,2,3,1,0:T(8,128)(2,1)}), bf16[64,1,64,2,512]{4,2,3,1,0:T(8,128)(2,1)}, u32[]{:S(2)}, u32[]{:S(2)}) %all-to-all-start) | async-done | bytes 8388640 | tf_op jit(solution)/shard_map/all_to_all | solution.py:96
  211.1 2.1 broadcast_in_dim.29
  213.2 4.2 all-to-all-start.1
  217.8 1.8 convolution_bitcast_fusion
  220.0 43.9 %conditional.1 = ((f32[2,8,64]{2,1,0:T(8,128)S(1)}, f32[64,2,8,512]{3,0,2,1:T(8,128)})) conditional(s32[]{:T(128)} %convert_element_type.74, (f32[2,8,64]{2,1,0:T(8,128)S(1)}, f32[64,2,8,512]{3,0,2,1:T(8,128)}) %tuple.12, (s32[64]{0:T(128)S(1)}, s32[1,2]{1,0:T(1,128)}, bf16[64,1,64,2,512]{4,2,3,1,0:T(8,128)(2,1)}, bf16[64,2,8,512]{3,2,1,0:T(8,128)(2,1)}, ...), branch_computations={%region_3.0_spmd, %region_4.7_spmd} | conditional | flops 8637918208 | bytes 142156160 | solution.py:99
  221.5 7.7 %copy.57 = bf16[64,1,64,2,512]{4,2,0,3,1:T(8,128)(2,1)} copy(bf16[64,1,64,2,512]{4,2,3,1,0:T(8,128)(2,1)} %get-tuple-element.52) | data formatting | bytes 16777216 | tf_op jit(solution)/shard_map
  229.2 15.3 %fusion.2 = (f32[2,8,64]{2,1,0:T(8,128)}, f32[2,4096,64,8]{1,2,3,0:T(8,128)}) fusion(pred[2,64,4096]{2,1,0:T(8,128)(4,1)S(1)} %broadcast_and_fusion, bf16[4096,2,512,1]{2,0,3,1:T(8,128)(2,1)} %bitcast.148, bf16[64,2,8,512]{3,2,1,0:T(8,128)(2,1)} %get-tuple-element.57), kind=kOutput, calls=%fused_computation.4 | convolution fusion | flops 4307549184 | bytes 26742784 | tf_op jit(solution)/shard_map/cond/branch_1_fun/tshl,jsl->shtj/dot_general | solution.py:74
  245.3 9.1 %fusion.1 = f32[2,8,64]{2,1,0:T(8,128)S(1)} fusion(f32[2,4096,64,8]{1,2,3,0:T(8,128)} %get-tuple-element.61, f32[2,8,64]{2,1,0:T(8,128)S(1)} %get-tuple-element.59, pred[2,64,4096]{2,1,0:T(8,128)(4,1)S(1)} %broadcast_and_fusion), kind=kLoop, calls=%fused_computation.3 | loop fusion | flops 16776192 | bytes 17309696 | tf_op jit(solution)/shard_map/cond/branch_1_fun/reduce_sum | solution.py:84
  254.4 8.3 %bitcast_add_fusion = f32[64,2,8,512]{3,0,2,1:T(8,128)S(1)} fusion(f32[64,2,8,512]{3,0,2,1:T(8,128)S(1)} %copy-done.4, bf16[4096,2,512,1]{2,0,3,1:T(8,128)(2,1)S(1)} %bitcast.149, f32[2,4096,64,8]{1,2,3,0:T(8,128)} %get-tuple-element.61, f32[2,8,64]{2,1,0:T(8,128)S(1)} %get-tuple-element.59, pred[2,64,4096]{2,1,0:T(8,128)(4,1)S(1)} %broadcast_and_fusion, ...), kind=kOutput, calls=%fused_computation.10 | convolution fusion | flops 4312793088 | bytes 29892608 | tf_op jit(solution)/shard_map/cond/branch_1_fun/shtj,jsl->tshl/dot_general | solution.py:85
  262.7 1.3 copy-done.5
  264.0 2.4 fusion.44
  266.5 3.3 multiply_reduce_fusion
  270.8 3.0 convolution_convert_fusion
  273.9 6.0 %reshape.137 = bf16[64,1,14,2048]{3,2,0,1:T(8,128)(2,1)} reshape(bf16[896,2048]{1,0:T(8,128)(2,1)} %convolution_convert_fusion) | data formatting | bytes 7340032 | tf_op jit(solution)/shard_map/reshape | solution.py:144
  279.9 102.2 %all_to_all.20 = bf16[64,1,14,2048]{3,2,1,0:T(8,128)(2,1)S(1)} all-to-all(bf16[64,1,14,2048]{3,2,1,0:T(8,128)(2,1)} %bitcast.147), channel_id=1, replica_groups=mesh['dp'=4,'expert'=64] {'expert'}, dimensions={0} | all-to-all | bytes 7340032 | tf_op jit(solution)/shard_map/all_to_all | solution.py:145
  382.1 1.9 copy-done.3
  384.0 8.7 %fusion.18 = f32[64,14,704]{2,0,1:T(8,128)} fusion(bf16[64,1,14,2048]{3,2,1,0:T(8,128)(2,1)S(1)} %all_to_all.20, bf16[1,2048,704]{1,2,0:T(8,128)(2,1)S(1)} %copy-done.11), kind=kOutput, calls=%fused_computation.23 | convolution fusion | flops 2583691264 | bytes 9076736 | tf_op jit(solution)/shard_map/necd,edf->necf/dot_general | solution.py:146
  392.7 12.9 %convert_bitcast_fusion = bf16[64,1,14,2048]{3,0,2,1:T(8,128)(2,1)} fusion(bf16[1,704,2048]{2,1,0:T(8,128)(2,1)S(1)} %copy-done, bf16[1,2048,704]{1,2,0:T(8,128)(2,1)} %param.26, bf16[64,1,14,2048]{3,2,1,0:T(8,128)(2,1)} %copy-done.3, f32[64,14,704]{2,0,1:T(8,128)} %fusion.18), kind=kOutput, calls=%fused_computation.25 | convolution fusion | flops 5173002240 | bytes 15630336 | tf_op jit(solution)/shard_map/necf,efd->necd/dot_general | solution.py:149
  405.6 6.0 %copy.70 = bf16[64,1,14,2048]{3,2,1,0:T(8,128)(2,1)} copy(bf16[64,1,14,2048]{3,0,2,1:T(8,128)(2,1)} %convert_bitcast_fusion) | data formatting | bytes 7340032 | tf_op jit(solution)/shard_map/convert_element_type | solution.py:149
  411.6 6.2 %all-to-all-start.3 = ((bf16[64,1,14,2048]{3,2,1,0:T(8,128)(2,1)}), bf16[64,1,14,2048]{3,2,1,0:T(8,128)(2,1)}, u32[]{:S(2)}, u32[]{:S(2)}) async-start(bf16[64,1,14,2048]{3,2,1,0:T(8,128)(2,1)} %copy.70), calls=%async_computation.3 | async-start | bytes 8388608 | tf_op jit(solution)/shard_map/all_to_all | solution.py:152
  418.0 1.0 select_reduce_fusion
  419.0 94.6 %all-to-all-done.3 = bf16[64,1,14,2048]{3,2,1,0:T(8,128)(2,1)} async-done(((bf16[64,1,14,2048]{3,2,1,0:T(8,128)(2,1)}), bf16[64,1,14,2048]{3,2,1,0:T(8,128)(2,1)}, u32[]{:S(2)}, u32[]{:S(2)}) %all-to-all-start.3) | async-done | bytes 3670048 | tf_op jit(solution)/shard_map/all_to_all | solution.py:152
  513.7 6.0 %reshape.143 = bf16[896,2048]{1,0:T(8,128)(2,1)} reshape(bf16[64,1,14,2048]{3,2,1,0:T(8,128)(2,1)} %all-to-all-done.3) | data formatting | bytes 7340032 | tf_op jit(solution)/shard_map/reshape | solution.py:153
  519.6 3.1 fusion.30
  522.8 1.1 reshape.144
  (52 shorter events, 6.4 us)
Async XLA Ops:
  6.5 386.1 %copy-start = (bf16[1,704,2048]{2,1,0:T(8,128)(2,1)S(1)}, bf16[1,704,2048]{2,1,0:T(8,128)(2,1)}, u32[]{:S(2)}) copy-start(bf16[1,704,2048]{2,1,0:T(8,128)(2,1)} %param.27) | copy-start | bytes 8650756
  11.9 14.2 %copy-start.8 = (s32[1,64,2,6]{1,2,3,0:T(2,128)S(1)}, s32[1,64,2,6]{1,2,3,0:T(2,128)}, u32[]{:S(2)}) copy-start(s32[1,64,2,6]{1,2,3,0:T(2,128)} %param.20) | copy-start | bytes 9220
  11.9 199.2 %all-to-all-start = ((bf16[64,1,64,2,512]{4,2,3,1,0:T(8,128)(2,1)}), bf16[64,1,64,2,512]{4,2,3,1,0:T(8,128)(2,1)}, u32[]{:S(2)}, u32[]{:S(2)}) async-start(bf16[64,1,64,2,512]{4,2,3,1,0:T(8,128)(2,1)} %stack.2), calls=%async_computation | async-start | bytes 16777216 | tf_op jit(solution)/shard_map/all_to_all | solution.py:96
  25.4 5.1 copy-start.6
  25.4 241.2 %all-gather.2.cloned.1.call-start = ((), (), s32[]{:S(2)}) async-start(), calls=%async_computation.4 | async-start | bytes 5242880 | tf_op jit(solution)/shard_map/all_gather | solution.py:115
  30.4 187.3 %copy-start.9 = (bf16[2048]{0:T(1024)(128)(2,1)S(1)}, bf16[2048]{0:T(1024)(128)(2,1)}, u32[]{:S(2)}) copy-start(bf16[2048]{0:T(1024)(128)(2,1)} %param.22) | copy-start | bytes 12292
  31.6 186.2 %copy-start.7 = (bf16[1,32,2,512]{3,2,1,0:T(2,128)(2,1)S(1)}, bf16[1,32,2,512]{3,2,1,0:T(2,128)(2,1)}, u32[]{:S(2)}) copy-start(bf16[1,32,2,512]{3,2,1,0:T(2,128)(2,1)} %param.18) | copy-start | bytes 196612
  213.2 50.8 %all-to-all-start.1 = ((bf16[4,2,512,128]{3,2,1,0:T(8,128)(2,1)}), bf16[4,2,512,128]{3,2,1,0:T(8,128)(2,1)}, u32[]{:S(2)}, u32[]{:S(2)}) async-start(bf16[4,2,512,128]{3,2,1,0:T(8,128)(2,1)} %broadcast_in_dim.29), calls=%async_computation.1 | async-start | bytes 2097152 | tf_op jit(solution)/shard_map/all_to_all | solution.py:12
  245.2 9.1 %copy-start.2 = (bf16[64,1,64,2,512]{4,2,0,3,1:T(8,128)(2,1)S(1)}, bf16[64,1,64,2,512]{4,2,0,3,1:T(8,128)(2,1)}, u32[]{:S(2)}) copy-start(bf16[64,1,64,2,512]{4,2,0,3,1:T(8,128)(2,1)} %copy.57) | copy-start | bytes 25165828 | tf_op jit(solution)/shard_map/cond
  245.2 9.1 %copy-start.4 = (f32[64,2,8,512]{3,0,2,1:T(8,128)S(1)}, f32[64,2,8,512]{3,0,2,1:T(8,128)}, u32[]{:S(2)}) copy-start(f32[64,2,8,512]{3,0,2,1:T(8,128)} %get-tuple-element.29) | copy-start | bytes 6291460 | tf_op jit(solution)/shard_map/cond
  262.7 1.3 copy-start.5
  269.8 1.0 copy-start.1
  279.9 104.1 %copy-start.11 = (bf16[1,2048,704]{1,2,0:T(8,128)(2,1)S(1)}, bf16[1,2048,704]{1,2,0:T(8,128)(2,1)}, u32[]{:S(2)}) copy-start(bf16[1,2048,704]{1,2,0:T(8,128)(2,1)} %param.25) | copy-start | bytes 8650756
  382.1 1.9 copy-start.3
  411.6 6.2 %copy-start.10 = (bf16[1,64,2,6]{1,2,3,0:T(2,128)(2,1)S(1)}, bf16[1,64,2,6]{1,2,3,0:T(2,128)(2,1)}, u32[]{:S(2)}) copy-start(bf16[1,64,2,6]{1,2,3,0:T(2,128)(2,1)} %param.21) | copy-start | bytes 4612
  411.6 102.0 %all-to-all-start.3 = ((bf16[64,1,14,2048]{3,2,1,0:T(8,128)(2,1)}), bf16[64,1,14,2048]{3,2,1,0:T(8,128)(2,1)}, u32[]{:S(2)}, u32[]{:S(2)}) async-start(bf16[64,1,14,2048]{3,2,1,0:T(8,128)(2,1)} %copy.70), calls=%async_computation.3 | async-start | bytes 8388608 | tf_op jit(solution)/shard_map/all_to_all | solution.py:152
Sparse Core Ops, SparseCore 0:
  28.0 51.5 all-gather.1
